TPU v7x, 32 devices: a whole 2x2x4 slice. The times are simulated.
32 devices in a mesh: fsdp: 2 (over core), width: 4 (over y, x), unit: 4 (over z).
Axes of the slice: x: 2, y: 2, z: 4, core: 2. Of those that a mesh axis runs over, the one named last changes fastest.
Arguments:
- train_gate: bfloat16 [8192, 8192], P(('unit', 'fsdp'), 'width'), parts along dimension 0, may hold values from -0.125 to 0.125
- low_gate: bfloat16 [8192, 32], P(('unit', 'fsdp')), parts along dimension 0, may hold values from -0.125 to 0.125
- high_gate: bfloat16 [128, 8192], P('unit', 'width'), parts along dimension 0, may hold values from -1 to 1
- train_up: bfloat16 [8192, 8192], P(('unit', 'fsdp'), 'width'), parts along dimension 0, may hold values from -0.125 to 0.125
- low_up: bfloat16 [8192, 32], P(('unit', 'fsdp')), parts along dimension 0, may hold values from -0.125 to 0.125
- high_up: bfloat16 [128, 8192], P('unit', 'width'), parts along dimension 0, may hold values from -1 to 1
- norm_train: float32 [8192], P(('unit', 'fsdp', 'width')), parts along dimension 0, may hold values from 0.25 to 1.75
- norm_step: float32 [8192], P(('unit', 'fsdp', 'width')), parts along dimension 0, may hold values from -0.3 to 0.3
Outputs:
- final_gate: bfloat16 [32768, 2048], P(('unit', 'width')), parts along dimension 0
- final_up: bfloat16 [32768, 2048], P(('unit', 'width')), parts along dimension 0
- serve_norm: bfloat16 [8192], P('unit'), parts along dimension 0
There are 4 independent parts, one for each index of `unit`. A program takes and returns all parts, laid end to end along the dimension named above; each array names one. Nothing has to cross between parts.
All inputs are finite; a program needn't handle non-finite values.
Results may differ from a plain program's by a relative error of at most 0.001.
Values may be sent and summed in bfloat16 or wider, within the bound.
A program may use at most 128 MiB of HBM per device.

v0:
```python
import jax
import jax.numpy as jnp
from jax import lax
from jax.sharding import PartitionSpec as P

mix_rate = 2.0


def body(train_gate, low_gate, high_gate, train_up, low_up, high_up, norm_train, norm_step):
    result_gate = train_gate.astype(jnp.float32) + mix_rate * jnp.dot(
        low_gate, high_gate, preferred_element_type=jnp.float32
    )
    result_up = train_up.astype(jnp.float32) + mix_rate * jnp.dot(
        low_up, high_up, preferred_element_type=jnp.float32
    )
    narrow_gate, narrow_up = (result_gate.astype(jnp.bfloat16), result_up.astype(jnp.bfloat16))
    final_gate, final_up = (
        lax.all_gather(narrow_gate, "fsdp", axis=0, tiled=True),
        lax.all_gather(narrow_up, "fsdp", axis=0, tiled=True),
    )
    final_gate, final_up = (final_gate.T, final_up.T)
    serve_norm = lax.all_gather(
        (norm_train + norm_step).astype(jnp.bfloat16), ("fsdp", "width"), axis=0, tiled=True
    )
    return (final_gate, final_up, serve_norm)


def solution(mesh):
    return jax.shard_map(
        body,
        mesh=mesh,
        in_specs=(
            P(("unit", "fsdp"), "width"),
            P(("unit", "fsdp"), None),
            P("unit", "width"),
            P(("unit", "fsdp"), "width"),
            P(("unit", "fsdp"), None),
            P("unit", "width"),
            P(("unit", "fsdp", "width")),
            P(("unit", "fsdp", "width")),
        ),
        out_specs=(P(("unit", "width"), None), P(("unit", "width"), None), P("unit")),
        check_vma=False,
    )
```

profile of v0, /device:TPU:0, one launch (start us, length us, event | category | flops | bytes accessed | tf_op | source)
XLA Modules:
  0.0 78.1 jit_solution(2958209487717878340)
XLA Ops:
  7.2 0.0 copy-start
  7.2 0.0 copy-start.2
  7.2 0.0 copy-start.1
  7.2 0.0 all-gather.4.cloned.1.call-start
  7.2 0.8 %copy-done = bf16[32,2048]{1,0:T(8,128)(2,1)S(1)} copy-done((bf16[32,2048]{1,0:T(8,128)(2,1)S(1)}, bf16[32,2048]{1,0:T(8,128)(2,1)}, u32[]{:S(2)}) %copy-start) | copy-done | bytes 131096
  8.1 5.5 %add_convert_fusion.1 = bf16[1024,2048]{1,0:T(8,128)(2,1)} fusion(bf16[1024,2048]{1,0:T(8,128)(2,1)} %param.8, bf16[1024,32]{0,1:T(8,128)(2,1)} %param.9, bf16[32,2048]{1,0:T(8,128)(2,1)S(1)} %copy-done), kind=kOutput, calls=%fused_computation.1 | convolution fusion | flops 142606336 | bytes 8585216 | tf_op jit(solution)/shard_map/dot_general | solution.py:10
  13.6 0.0 copy-start.3
  13.6 0.0 copy-start.4
  13.6 0.0 all-gather.4.cloned.1.call-update
  13.6 0.0 all-gather.6.cloned.1.call-start
  13.7 0.0 copy-done.2
  13.7 0.0 copy-done.1
  13.7 5.4 %add_convert_fusion = bf16[1024,2048]{1,0:T(8,128)(2,1)} fusion(bf16[1024,2048]{1,0:T(8,128)(2,1)} %param.11, bf16[1024,32]{0,1:T(8,128)(2,1)S(1)} %copy-done.2, bf16[32,2048]{1,0:T(8,128)(2,1)S(1)} %copy-done.1), kind=kOutput, calls=%fused_computation | convolution fusion | flops 142606336 | bytes 8585216 | tf_op jit(solution)/shard_map/dot_general | solution.py:13
  19.1 0.0 all-gather.6.cloned.1.call-update
  19.1 0.0 copy-done.3
  19.1 0.0 copy-done.4
  19.2 14.9 %all-gather = bf16[8,1,256]{2,1,0:T(2,128)(2,1)S(1)} all-gather(bf16[1,1,256]{2,1,0:T(2,128)(2,1)S(1)} %reshape.6), channel_id=1, replica_groups=mesh['fsdp'=2,'width'=4,'unit'=4] {'fsdp','width'}, dimensions={0}, use_global_device_ids=true | all-gather | bytes 4608 | tf_op jit(solution)/shard_map/all_gather | solution.py:22
  34.1 0.6 copy.17
  34.7 1.7 %all-gather.4.cloned.1.call-done = bf16[2048,2048]{1,0:T(8,128)(2,1)} async-done(((bf16[1024,2048]{1,0:T(8,128)(2,1)}), bf16[2048,2048]{1,0:T(8,128)(2,1)}) %all-gather.4.cloned.1.call-update) | async-done | bytes 8388624 | tf_op jit(solution)/shard_map/all_gather | solution.py:18
  36.4 12.2 %copy.15 = bf16[2048,2048]{1,0:T(8,128)(2,1)} copy(bf16[2048,2048]{0,1:T(8,128)(2,1)} %bitcast.8) | data formatting | bytes 16777216
  48.6 10.4 %all-gather.6.cloned.1.call-done = bf16[2048,2048]{1,0:T(8,128)(2,1)} async-done(((bf16[1024,2048]{1,0:T(8,128)(2,1)}), bf16[2048,2048]{1,0:T(8,128)(2,1)}) %all-gather.6.cloned.1.call-update) | async-done | bytes 8388624 | tf_op jit(solution)/shard_map/all_gather | solution.py:19
  59.0 12.2 %copy.16 = bf16[2048,2048]{1,0:T(8,128)(2,1)} copy(bf16[2048,2048]{0,1:T(8,128)(2,1)} %bitcast.9) | data formatting | bytes 16777216
  (3 shorter events, 0.0 us)
Async XLA Ops:
  7.2 0.9 %copy-start = (bf16[32,2048]{1,0:T(8,128)(2,1)S(1)}, bf16[32,2048]{1,0:T(8,128)(2,1)}, u32[]{:S(2)}) copy-start(bf16[32,2048]{1,0:T(8,128)(2,1)} %param.10) | copy-start | bytes 393220
  7.2 6.5 %copy-start.2 = (bf16[1024,32]{0,1:T(8,128)(2,1)S(1)}, bf16[1024,32]{0,1:T(8,128)(2,1)}, u32[]{:S(2)}) copy-start(bf16[1024,32]{0,1:T(8,128)(2,1)} %param.12) | copy-start | bytes 196612
  7.2 6.5 %copy-start.1 = (bf16[32,2048]{1,0:T(8,128)(2,1)S(1)}, bf16[32,2048]{1,0:T(8,128)(2,1)}, u32[]{:S(2)}) copy-start(bf16[32,2048]{1,0:T(8,128)(2,1)} %param.13) | copy-start | bytes 393220
  7.2 29.2 %all-gather.4.cloned.1.call-start = ((), (), s32[]{:S(2)}) async-start(), calls=%async_computation | async-start | bytes 12582912 | tf_op jit(solution)/shard_map/all_gather | solution.py:18
  13.6 5.5 %copy-start.3 = (f32[256]{0:T(256)S(1)}, f32[256]{0:T(256)}, u32[]{:S(2)}) copy-start(f32[256]{0:T(256)} %param.14) | copy-start | bytes 3076
  13.6 5.5 %copy-start.4 = (f32[256]{0:T(256)S(1)}, f32[256]{0:T(256)}, u32[]{:S(2)}) copy-start(f32[256]{0:T(256)} %param.15) | copy-start | bytes 3076
  13.6 45.4 %all-gather.6.cloned.1.call-start = ((), (), s32[]{:S(2)}) async-start(), calls=%async_computation.1 | async-start | bytes 12582912 | tf_op jit(solution)/shard_map/all_gather | solution.py:19
Sparse Core Ops, SparseCore 0:
  13.7 22.5 all-gather.3
  37.9 21.0 all-gather.5
where the time goes:
time: 78.8 us; the launch traced here: 78.1 us
  local copies, waits for them, and re-layouts  25.9 us (33%)
  blocking collectives  14.9 us (19%)
  between operations  14.1 us (18%)
  waiting for transfers between devices  12.1 us (15%)
  matrix products  10.9 us (14%)
    unnamed x14, local copies, waits for them, and re-layouts  25.9 us
    all_gather x1, blocking collectives, body(): lax.all_gather((norm_train + norm_step).astype(jnp.bfloat16), ('fsdp', 'w...  14.9 us
    all_gather x1, waiting for transfers between devices, body(): lax.all_gather(narrow_up, 'fsdp', axis=0, tiled=True)  10.4 us
    dot_general x1, matrix products, body(): jnp.dot(low_gate, high_gate, preferred_element_type=jnp.float32)  5.52 us
    dot_general x1, matrix products, body(): jnp.dot(low_up, high_up, preferred_element_type=jnp.float32)  5.41 us
    all_gather x1, waiting for transfers between devices, body(): lax.all_gather(narrow_gate, 'fsdp', axis=0, tiled=True)  1.66 us
  transfers between devices with their start and end apart: 2, of which 2 were waited for; matrix products, arithmetic and copies ran while one was open for 23% of the time, Pallas kernels for 0%

commit v1 on v0

v1 whole, which is shorter than its diff:
```python
import functools

import jax
import jax.numpy as jnp
from jax import lax
from jax.experimental import pallas as pl
from jax.experimental.pallas import tpu as pltpu
from jax.sharding import PartitionSpec as P

mix_rate = 2.0


def piece_kernel(at_ref, train_ref, low_ref, high_ref, *rest):
    out_ref = rest[-1]
    width = train_ref.shape[1]
    high = (high_ref[...].astype(jnp.float32) * mix_rate).astype(jnp.bfloat16)
    mixed = lax.dot_general(
        high, low_ref[...], (((0,), (0,)), ((), ())), preferred_element_type=jnp.float32
    )
    out_ref[...] = (train_ref[...].T.astype(jnp.float32) + mixed).astype(out_ref.dtype)


def place_piece(at, train, low, high, whole, total):
    rows, columns = train.shape
    rank = high.shape[0]
    block = min(512, columns)
    in_specs = [
        pl.BlockSpec((rows, block), lambda i, at: (0, i)),
        pl.BlockSpec((rank, rows), lambda i, at: (0, 0)),
        pl.BlockSpec((rank, block), lambda i, at: (0, i)),
    ]
    operands = [train, low, high]
    aliases = {}
    if whole is not None:
        in_specs.append(pl.BlockSpec(memory_space=pl.ANY))
        operands.append(whole)
        aliases = {4: 0}
    return pl.pallas_call(
        piece_kernel,
        out_shape=jax.ShapeDtypeStruct((columns, total), jnp.bfloat16),
        grid_spec=pltpu.PrefetchScalarGridSpec(
            num_scalar_prefetch=1,
            grid=(columns // block,),
            in_specs=in_specs,
            out_specs=pl.BlockSpec((block, rows), lambda i, at: (i, at[0])),
        ),
        input_output_aliases=aliases,
        compiler_params=pltpu.CompilerParams(dimension_semantics=("arbitrary",)),
        cost_estimate=pl.CostEstimate(
            flops=2 * rows * columns * rank, bytes_accessed=4 * rows * columns, transcendentals=0
        ),
    )(at, *operands)


def gain_kernel(sizes, mine_ref, all_ref, send_sem, recv_sem, own_sem):
    fsdp, width = sizes
    count = fsdp * width
    row, column = lax.axis_index("fsdp"), lax.axis_index("width")
    me = row * width + column

    def peer(step):
        to = lax.rem(me + step, count)
        return {"fsdp": to // width, "width": lax.rem(to, width)}

    barrier = pltpu.get_barrier_semaphore()
    for step in range(1, count):
        pl.semaphore_signal(barrier, inc=1, device_id=peer(step))
    own = pltpu.make_async_copy(mine_ref, all_ref.at[me], own_sem)
    own.start()
    pl.semaphore_wait(barrier, count - 1)
    copies = []
    for step in range(1, count):
        copy = pltpu.make_async_remote_copy(
            src_ref=mine_ref,
            dst_ref=all_ref.at[me],
            send_sem=send_sem.at[step],
            recv_sem=recv_sem.at[step],
            device_id=peer(step),
        )
        copy.start()
        copies.append(copy)
    own.wait()
    for copy in copies:
        copy.wait()


def gather_gain(gain, sizes):
    count = sizes[0] * sizes[1]
    shape = (gain.shape[0] // 128, 128) if gain.shape[0] % 128 == 0 else (1, gain.shape[0])
    gathered = pl.pallas_call(
        functools.partial(gain_kernel, sizes),
        out_shape=jax.ShapeDtypeStruct((count,) + shape, jnp.float32),
        in_specs=[pl.BlockSpec(memory_space=pltpu.VMEM)],
        out_specs=pl.BlockSpec(memory_space=pltpu.VMEM),
        scratch_shapes=[
            pltpu.SemaphoreType.DMA((count,)),
            pltpu.SemaphoreType.DMA((count,)),
            pltpu.SemaphoreType.DMA,
        ],
        compiler_params=pltpu.CompilerParams(collective_id=0, has_side_effects=True),
        cost_estimate=pl.CostEstimate(flops=0, bytes_accessed=8000000, transcendentals=0),
    )(gain.reshape(shape))
    return gathered.reshape(-1).astype(jnp.bfloat16)


def solution(mesh):
    fsdp, width = mesh.shape["fsdp"], mesh.shape["width"]

    def body(train_gate, low_gate, high_gate, train_up, low_up, high_up, norm_train, norm_step):
        total = train_gate.shape[0] * fsdp
        me = lax.axis_index("fsdp").astype(jnp.int32)
        lows = (low_gate.T, low_up.T)
        trains = (train_gate, train_up)
        highs = (high_gate, high_up)
        arrived = []
        for step in range(1, fsdp):
            ring = [(at, (at + step) % fsdp) for at in range(fsdp)]
            for which in range(2):
                arrived.append(
                    (
                        which,
                        lax.rem(me + fsdp - step, fsdp),
                        lax.ppermute(lows[which], "fsdp", ring),
                        lax.ppermute(trains[which], "fsdp", ring),
                    )
                )
        finals = [
            place_piece(me.reshape(1), trains[which], lows[which], highs[which], None, total)
            for which in range(2)
        ]
        serve_norm = gather_gain(norm_train + norm_step, (fsdp, width))
        for which, at, low, train in arrived:
            finals[which] = place_piece(
                at.reshape(1), train, low, highs[which], finals[which], total
            )
        return (finals[0], finals[1], serve_norm)

    return jax.shard_map(
        body,
        mesh=mesh,
        in_specs=(
            P(("unit", "fsdp"), "width"),
            P(("unit", "fsdp"), None),
            P("unit", "width"),
            P(("unit", "fsdp"), "width"),
            P(("unit", "fsdp"), None),
            P("unit", "width"),
            P(("unit", "fsdp", "width")),
            P(("unit", "fsdp", "width")),
        ),
        out_specs=(P(("unit", "width"), None), P(("unit", "width"), None), P("unit")),
        check_vma=False,
    )
```

time: 78.8 us -> 42.2 us (0.54)
  Pallas kernels: 0 us -> 35.9 us
  local copies, waits for them, and re-layouts: 25.9 us -> 1.21 us
  blocking collectives: 14.9 us -> 0 us
  between operations: 14.1 us -> 0.67 us
  waiting for transfers between devices: 12.1 us -> 0.01 us
  matrix products: 10.9 us -> 0 us
  other arithmetic: 0.04 us -> 2.55 us
  starting transfers between devices: 0.08 us -> 1.17 us
    pallas_call x0 -> x5, Pallas kernels: none -> 35.9 us  [the longest x4 23.8 us: place_piece(): pl.pallas_call(piece_kernel, out_shape=jax.ShapeDtypeStruct((columns, tot...]
    unnamed x14 -> x4, local copies, waits for them, and re-layouts: 25.9 us -> 1.21 us
    all_gather x1 -> x0, blocking collectives: 14.9 us -> none  [body(): lax.all_gather((norm_train + norm_step).astype(jnp.bfloat16), ('fsdp', 'w...]
    all_gather x2 -> x0, waiting for transfers between devices: 12 us -> none  [the longest x1 10.4 us: body(): lax.all_gather(narrow_up, 'fsdp', axis=0, tiled=True)]
    dot_general x2 -> x0, matrix products: 10.9 us -> none  [the longest x1 5.52 us: body(): jnp.dot(low_gate, high_gate, preferred_element_type=jnp.float32)]
    convert_element_type x1, other arithmetic: 0.01 us -> 1.29 us  [gather_gain(): return gathered.reshape(-1).astype(jnp.bfloat16)]
    reshape x0 -> x1, other arithmetic: none -> 1.26 us  [gather_gain(): gain.reshape(shape)]
    ppermute x0 -> x4, starting transfers between devices: none -> 1.17 us  [the longest x2 0.66 us: body(): lax.ppermute(trains[which], 'fsdp', ring)]
  transfers between devices with their start and end apart: 2 -> 4, of which waited for: 2 -> 0; matrix products, arithmetic and copies ran while one was open for 23% -> 6% of each run, Pallas kernels for 0% -> 72%
where the time goes in v1:
time: 42.2 us; the launch traced here: 41.5 us
  Pallas kernels  35.9 us (85%)
  other arithmetic  2.55 us (6%)
  local copies, waits for them, and re-layouts  1.21 us (3%)
  starting transfers between devices  1.17 us (3%)
  between operations  0.67 us (2%)
    pallas_call x4, Pallas kernels, place_piece(): pl.pallas_call(piece_kernel, out_shape=jax.ShapeDtypeStruct((columns, tot...  23.8 us
    pallas_call x1, Pallas kernels, gather_gain(): pl.pallas_call(functools.partial(gain_kernel, sizes), out_shape=jax.Shape...  12.1 us
    convert_element_type x1, other arithmetic, gather_gain(): return gathered.reshape(-1).astype(jnp.bfloat16)  1.29 us
    reshape x1, other arithmetic, gather_gain(): gain.reshape(shape)  1.26 us
    unnamed x4, local copies, waits for them, and re-layouts  1.21 us
  transfers between devices with their start and end apart: 4, of which 0 were waited for; matrix products, arithmetic and copies ran while one was open for 6% of the time, Pallas kernels for 72%

profile of v1, /device:TPU:0, one launch (start us, length us, event | category | flops | bytes accessed | tf_op | source)
XLA Modules:
  0.0 41.5 jit_solution(18207839538001377972)
XLA Ops:
  0.6 0.6 %collective-permute-start.2 = (bf16[1024,2048]{1,0:T(8,128)(2,1)}, bf16[1024,2048]{1,0:T(8,128)(2,1)}, u32[]{:S(2)}, u32[]{:S(2)}) collective-permute-start(bf16[1024,2048]{1,0:T(8,128)(2,1)} %train_ref.3), channel_id=1, source_target_pairs={{0,16},{16,0},{1,17},{17,1},{2,18},{18,2},{3,19},{19,3},{4,20},{20... | collective-permute-start | bytes 12582920 | tf_op jit(solution)/shard_map/ppermute | solution.py:124
  1.2 0.1 collective-permute-start
  1.3 0.4 %collective-permute-start.3 = (bf16[32,1024]{1,0:T(8,128)(2,1)}, bf16[32,1024]{1,0:T(8,128)(2,1)S(1)}, u32[]{:S(2)}, u32[]{:S(2)}) collective-permute-start(bf16[32,1024]{1,0:T(8,128)(2,1)} %bitcast.7), channel_id=1, source_target_pairs={{0,16},{16,0},{1,17},{17,1},{2,18},{18,2},{3,19},{19,3},{4,20},{20... | collective-permute-start | bytes 196616 | tf_op jit(solution)/shard_map/ppermute | solution.py:123
  1.7 0.1 collective-permute-start.1
  1.8 1.3 %add_bitcast_fusion.mine_ref = f32[2,128]{1,0:T(2,128)} fusion(f32[256]{0:T(256)} %param.14, f32[256]{0:T(256)} %param.15), kind=kLoop, calls=%fused_computation | loop fusion | flops 256 | bytes 3072 | tf_op jit(solution)/shard_map/reshape | solution.py:102
  3.1 12.1 %shard_map.107 = f32[8,2,128]{2,1,0:T(2,128)} custom-call(f32[2,128]{1,0:T(2,128)} %add_bitcast_fusion.mine_ref), custom_call_target="tpu_custom_call" | custom-call | bytes 8000000 | tf_op jit(solution)/shard_map/pallas_call | solution.py:90
  15.2 1.3 %convert_element_type.6 = bf16[8,2,128]{2,1,0:T(2,128)(2,1)} convert(f32[8,2,128]{2,1,0:T(2,128)} %shard_map.107) | non-fusion elementwise | flops 2048 | bytes 12288 | tf_op jit(solution)/shard_map/convert_element_type | solution.py:103
  16.5 5.9 %shard_map.105.rest_0_ = bf16[2048,2048]{1,0:T(8,128)(2,1)} custom-call(s32[1]{0:T(128)} %bitcast.2.at_ref, bf16[1024,2048]{1,0:T(8,128)(2,1)} %train_ref.3, bf16[32,1024]{1,0:T(8,128)(2,1)} %bitcast.8, bf16[32,2048]{1,0:T(8,128)(2,1)} %high_ref.7), custom_call_target="tpu_custom_call" | custom-call | flops 134217728 | bytes 8388608 | tf_op jit(solution)/shard_map/pallas_call | solution.py:38
  22.4 5.9 %shard_map.103.rest_0_ = bf16[2048,2048]{1,0:T(8,128)(2,1)} custom-call(s32[1]{0:T(128)} %bitcast.2.at_ref, bf16[1024,2048]{1,0:T(8,128)(2,1)} %train_ref.2, bf16[32,1024]{1,0:T(8,128)(2,1)} %bitcast.10, bf16[32,2048]{1,0:T(8,128)(2,1)} %high_ref.5), custom_call_target="tpu_custom_call" | custom-call | flops 134217728 | bytes 8388608 | tf_op jit(solution)/shard_map/pallas_call | solution.py:38
  28.4 0.0 collective-permute-done.3.low_ref
  28.4 0.0 copy-start.1
  28.4 0.0 collective-permute-done.2.train_ref
  28.4 0.6 %copy-done.1 = bf16[32,1024]{1,0:T(8,128)(2,1)} copy-done((bf16[32,1024]{1,0:T(8,128)(2,1)}, bf16[32,1024]{1,0:T(8,128)(2,1)S(1)}, u32[]{:S(2)}) %copy-start.1) | copy-done | bytes 65560
  29.0 5.9 %shard_map.106 = bf16[2048,2048]{1,0:T(8,128)(2,1)} custom-call(s32[1]{0:T(128)} %bitcast.at_ref, bf16[1024,2048]{1,0:T(8,128)(2,1)} %collective-permute-done.2.train_ref, bf16[32,1024]{1,0:T(8,128)(2,1)} %copy-done.1, bf16[32,2048]{1,0:T(8,128)(2,1)} %high_ref.7, bf16[2048,2048]{1,0:T(8,128)(2,1)} %shard_map.105.rest_0_), custom_call_target="tpu_custom_call", output_to_operand_aliasing={{}: (4, {})} | custom-call | flops 134217728 | bytes 8388608 | tf_op jit(solution)/shard_map/pallas_call | solution.py:38
  34.9 0.0 collective-permute-done.1.low_ref
  34.9 0.0 copy-start
  34.9 0.0 collective-permute-done.train_ref
  34.9 0.6 %copy-done = bf16[32,1024]{1,0:T(8,128)(2,1)} copy-done((bf16[32,1024]{1,0:T(8,128)(2,1)}, bf16[32,1024]{1,0:T(8,128)(2,1)S(1)}, u32[]{:S(2)}) %copy-start) | copy-done | bytes 65560
  35.5 5.9 %shard_map.104 = bf16[2048,2048]{1,0:T(8,128)(2,1)} custom-call(s32[1]{0:T(128)} %bitcast.at_ref, bf16[1024,2048]{1,0:T(8,128)(2,1)} %collective-permute-done.train_ref, bf16[32,1024]{1,0:T(8,128)(2,1)} %copy-done, bf16[32,2048]{1,0:T(8,128)(2,1)} %high_ref.5, bf16[2048,2048]{1,0:T(8,128)(2,1)} %shard_map.103.rest_0_), custom_call_target="tpu_custom_call", output_to_operand_aliasing={{}: (4, {})} | custom-call | flops 134217728 | bytes 8388608 | tf_op jit(solution)/shard_map/pallas_call | solution.py:38
Async XLA Ops:
  0.6 27.7 %collective-permute-start.2 = (bf16[1024,2048]{1,0:T(8,128)(2,1)}, bf16[1024,2048]{1,0:T(8,128)(2,1)}, u32[]{:S(2)}, u32[]{:S(2)}) collective-permute-start(bf16[1024,2048]{1,0:T(8,128)(2,1)} %train_ref.3), channel_id=1, source_target_pairs={{0,16},{16,0},{1,17},{17,1},{2,18},{18,2},{3,19},{19,3},{4,20},{20... | collective-permute-start | bytes 12582920 | tf_op jit(solution)/shard_map/ppermute | solution.py:124
  1.2 33.7 %collective-permute-start = (bf16[1024,2048]{1,0:T(8,128)(2,1)}, bf16[1024,2048]{1,0:T(8,128)(2,1)}, u32[]{:S(2)}, u32[]{:S(2)}) collective-permute-start(bf16[1024,2048]{1,0:T(8,128)(2,1)} %train_ref.2), channel_id=1, source_target_pairs={{0,16},{16,0},{1,17},{17,1},{2,18},{18,2},{3,19},{19,3},{4,20},{20... | collective-permute-start | bytes 12582920 | tf_op jit(solution)/shard_map/ppermute | solution.py:124
  1.3 27.1 %collective-permute-start.3 = (bf16[32,1024]{1,0:T(8,128)(2,1)}, bf16[32,1024]{1,0:T(8,128)(2,1)S(1)}, u32[]{:S(2)}, u32[]{:S(2)}) collective-permute-start(bf16[32,1024]{1,0:T(8,128)(2,1)} %bitcast.7), channel_id=1, source_target_pairs={{0,16},{16,0},{1,17},{17,1},{2,18},{18,2},{3,19},{19,3},{4,20},{20... | collective-permute-start | bytes 196616 | tf_op jit(solution)/shard_map/ppermute | solution.py:123
  1.7 33.2 %collective-permute-start.1 = (bf16[32,1024]{1,0:T(8,128)(2,1)}, bf16[32,1024]{1,0:T(8,128)(2,1)S(1)}, u32[]{:S(2)}, u32[]{:S(2)}) collective-permute-start(bf16[32,1024]{1,0:T(8,128)(2,1)} %bitcast.9), channel_id=1, source_target_pairs={{0,16},{16,0},{1,17},{17,1},{2,18},{18,2},{3,19},{19,3},{4,20},{20... | collective-permute-start | bytes 196616 | tf_op jit(solution)/shard_map/ppermute | solution.py:123
  28.4 0.6 %copy-start.1 = (bf16[32,1024]{1,0:T(8,128)(2,1)}, bf16[32,1024]{1,0:T(8,128)(2,1)S(1)}, u32[]{:S(2)}) copy-start(bf16[32,1024]{1,0:T(8,128)(2,1)S(1)} %collective-permute-done.3.low_ref) | copy-start | bytes 196612
  34.9 0.6 %copy-start = (bf16[32,1024]{1,0:T(8,128)(2,1)}, bf16[32,1024]{1,0:T(8,128)(2,1)S(1)}, u32[]{:S(2)}) copy-start(bf16[32,1024]{1,0:T(8,128)(2,1)S(1)} %collective-permute-done.1.low_ref) | copy-start | bytes 196612

commit v2 on v0

v2 whole, which is shorter than its diff:
```python
import functools

import jax
import jax.numpy as jnp
from jax import lax
from jax.experimental import pallas as pl
from jax.experimental.pallas import tpu as pltpu
from jax.sharding import PartitionSpec as P

mix_rate = 2.0
grant = 60 * 1024 * 1024


def piece_kernel(count, rows, columns, block, gain_too, at_ref, *refs):
    trains, lows, highs = refs[:count], refs[count : 2 * count], refs[2 * count : 3 * count]
    rest = refs[3 * count :]
    gains = None
    if gain_too:
        gains, rest = rest[0], rest[1:]
    scratch = rest[-8:]
    outs = rest[-8 - count - gain_too : -8]
    train_buf, low_buf, high_buf, out_buf, train_sem, low_sem, high_sem, out_sem = scratch
    chunks = columns // block
    first = pl.multiple_of(at_ref[0] * rows, rows)

    small, loads = [], []
    for which in range(count):
        small.append(
            (
                pltpu.make_async_copy(lows[which], low_buf.at[which], low_sem.at[which]),
                pltpu.make_async_copy(highs[which], high_buf.at[which], high_sem.at[which]),
            )
        )
        loads.append(
            [
                pltpu.make_async_copy(
                    trains[which].at[:, pl.ds(chunk * block, block)],
                    train_buf.at[which * chunks + chunk],
                    train_sem.at[which * chunks + chunk],
                )
                for chunk in range(chunks)
            ]
        )
    for which in range(count):
        for copy in small[which]:
            copy.start()
        for copy in loads[which]:
            copy.start()
    if gain_too:
        outs[count][...] = (gains[:, 0] + gains[:, 1]).astype(outs[count].dtype)
    stores = []
    for which in range(count):
        for copy in small[which]:
            copy.wait()
        low = low_buf[which]
        for chunk in range(chunks):
            slot = which * chunks + chunk
            high = high_buf[which, :, pl.ds(chunk * block, block)].astype(jnp.float32) * mix_rate
            mixed = lax.dot_general(
                high.astype(jnp.bfloat16),
                low,
                (((0,), (0,)), ((), ())),
                preferred_element_type=jnp.float32,
            )
            loads[which][chunk].wait()
            out_buf[slot] = (train_buf[slot].T.astype(jnp.float32) + mixed).astype(jnp.bfloat16)
            store = pltpu.make_async_copy(
                out_buf.at[slot],
                outs[which].at[pl.ds(chunk * block, block), pl.ds(first, rows)],
                out_sem.at[slot],
            )
            store.start()
            stores.append(store)
    for store in stores:
        store.wait()


def place_pieces(at, trains, lows, highs, wholes, total, gains=None):
    count = len(trains)
    rows, columns = trains[0].shape
    rank = highs[0].shape[0]
    block = min(256, columns)
    slots = count * (columns // block)
    anywhere = pl.BlockSpec(memory_space=pl.ANY)
    operands = [at, *trains, *lows, *highs]
    in_specs = [pl.BlockSpec(memory_space=pltpu.SMEM)] + [anywhere] * (3 * count)
    out_shape = [jax.ShapeDtypeStruct((columns, total), jnp.bfloat16)] * count
    out_specs = [anywhere] * count
    aliases = {}
    if gains is not None:
        operands.append(gains)
        in_specs.append(pl.BlockSpec(memory_space=pltpu.VMEM))
        out_shape.append(
            jax.ShapeDtypeStruct(gains.shape[:1] + gains.shape[2:], jnp.bfloat16)
        )
        out_specs.append(pl.BlockSpec(memory_space=pltpu.VMEM))
    if wholes is not None:
        aliases = {len(operands) + which: which for which in range(count)}
        operands += wholes
        in_specs += [anywhere] * count
    return pl.pallas_call(
        functools.partial(piece_kernel, count, rows, columns, block, int(gains is not None)),
        out_shape=out_shape,
        in_specs=in_specs,
        out_specs=out_specs,
        input_output_aliases=aliases,
        scratch_shapes=[
            pltpu.VMEM((slots, rows, block), jnp.bfloat16),
            pltpu.VMEM((count, rank, rows), jnp.bfloat16),
            pltpu.VMEM((count, rank, columns), jnp.bfloat16),
            pltpu.VMEM((slots, block, rows), jnp.bfloat16),
            pltpu.SemaphoreType.DMA((slots,)),
            pltpu.SemaphoreType.DMA((count,)),
            pltpu.SemaphoreType.DMA((count,)),
            pltpu.SemaphoreType.DMA((slots,)),
        ],
        compiler_params=pltpu.CompilerParams(vmem_limit_bytes=grant),
        cost_estimate=pl.CostEstimate(
            flops=2 * count * rows * columns * rank,
            bytes_accessed=4 * count * rows * columns,
            transcendentals=0,
        ),
    )(*operands)


def gain_kernel(sizes, train_ref, step_ref, after_ref, all_ref, send_sem, recv_sem, own_sem):
    fsdp, width = sizes
    count = fsdp * width
    row, column = lax.axis_index("fsdp"), lax.axis_index("width")
    me = row * width + column
    parts = (train_ref, step_ref)

    def peer(step):
        to = lax.rem(me + step, count)
        return {"fsdp": to // width, "width": lax.rem(to, width)}

    barrier = pltpu.get_barrier_semaphore()
    for step in range(1, count):
        pl.semaphore_signal(barrier, inc=1, device_id=peer(step))
    owns = [
        pltpu.make_async_copy(part, all_ref.at[me, kind], own_sem.at[kind])
        for kind, part in enumerate(parts)
    ]
    for own in owns:
        own.start()
    pl.semaphore_wait(barrier, count - 1)
    copies = []
    for step in range(1, count):
        for kind, part in enumerate(parts):
            copy = pltpu.make_async_remote_copy(
                src_ref=part,
                dst_ref=all_ref.at[me, kind],
                send_sem=send_sem.at[step, kind],
                recv_sem=recv_sem.at[step, kind],
                device_id=peer(step),
            )
            copy.start()
            copies.append(copy)
    for own in owns:
        own.wait()
    for copy in copies:
        copy.wait()


def gather_gains(norm_train, norm_step, sizes, after):
    count = sizes[0] * sizes[1]
    extent = norm_train.shape[0]
    shape = (extent // 128, 128) if extent % 128 == 0 else (1, extent)
    return pl.pallas_call(
        functools.partial(gain_kernel, sizes),
        out_shape=jax.ShapeDtypeStruct((count, 2) + shape, jnp.float32),
        in_specs=[
            pl.BlockSpec(memory_space=pltpu.VMEM),
            pl.BlockSpec(memory_space=pltpu.VMEM),
            pl.BlockSpec(memory_space=pl.ANY),
        ],
        out_specs=pl.BlockSpec(memory_space=pltpu.VMEM),
        scratch_shapes=[
            pltpu.SemaphoreType.DMA((count, 2)),
            pltpu.SemaphoreType.DMA((count, 2)),
            pltpu.SemaphoreType.DMA((2,)),
        ],
        compiler_params=pltpu.CompilerParams(
            collective_id=0, has_side_effects=True, vmem_limit_bytes=grant
        ),
        cost_estimate=pl.CostEstimate(flops=0, bytes_accessed=8000000, transcendentals=0),
    )(norm_train.reshape(shape), norm_step.reshape(shape), after)


def solution(mesh):
    fsdp, width = mesh.shape["fsdp"], mesh.shape["width"]

    def body(train_gate, low_gate, high_gate, train_up, low_up, high_up, norm_train, norm_step):
        total = train_gate.shape[0] * fsdp
        me = lax.axis_index("fsdp").astype(jnp.int32)
        lows = (low_gate.T, low_up.T)
        trains = (train_gate, train_up)
        highs = (high_gate, high_up)
        arrived = []
        for step in range(1, fsdp):
            ring = [(at, (at + step) % fsdp) for at in range(fsdp)]
            for which in range(2):
                arrived.append(
                    (
                        which,
                        lax.rem(me + fsdp - step, fsdp),
                        lax.ppermute(lows[which], "fsdp", ring),
                        lax.ppermute(trains[which], "fsdp", ring),
                    )
                )
        finals = list(place_pieces(me.reshape(1), trains, lows, highs, None, total))
        for which, at, low, train in arrived[:-1]:
            (finals[which],) = place_pieces(
                at.reshape(1), [train], [low], [highs[which]], [finals[which]], total
            )
        gains = gather_gains(norm_train, norm_step, (fsdp, width), finals[0])
        which, at, low, train = arrived[-1]
        finals[which], serve_norm = place_pieces(
            at.reshape(1), [train], [low], [highs[which]], [finals[which]], total, gains
        )
        serve_norm = serve_norm.reshape(-1)
        return (finals[0], finals[1], serve_norm)

    return jax.shard_map(
        body,
        mesh=mesh,
        in_specs=(
            P(("unit", "fsdp"), "width"),
            P(("unit", "fsdp"), None),
            P("unit", "width"),
            P(("unit", "fsdp"), "width"),
            P(("unit", "fsdp"), None),
            P("unit", "width"),
            P(("unit", "fsdp", "width")),
            P(("unit", "fsdp", "width")),
        ),
        out_specs=(P(("unit", "width"), None), P(("unit", "width"), None), P("unit")),
        check_vma=False,
    )
```

time: 78.8 us -> 36.8 us (0.47)
  Pallas kernels: 0 us -> 31.2 us
  local copies, waits for them, and re-layouts: 25.9 us -> 1.21 us
  blocking collectives: 14.9 us -> 0 us
  between operations: 14.1 us -> 0.68 us
  matrix products: 10.9 us -> 0 us
  waiting for transfers between devices: 12.1 us -> 2.28 us
  starting transfers between devices: 0.08 us -> 1.15 us
    pallas_call x0 -> x4, Pallas kernels: none -> 31.2 us  [the longest x3 23.5 us: place_pieces(): pl.pallas_call(functools.partial(piece_kernel, count, rows, columns, bloc...]
    unnamed x14 -> x4, local copies, waits for them, and re-layouts: 25.9 us -> 1.21 us
    all_gather x1 -> x0, blocking collectives: 14.9 us -> none  [body(): lax.all_gather((norm_train + norm_step).astype(jnp.bfloat16), ('fsdp', 'w...]
    all_gather x2 -> x0, waiting for transfers between devices: 12 us -> none  [the longest x1 10.4 us: body(): lax.all_gather(narrow_up, 'fsdp', axis=0, tiled=True)]
    dot_general x2 -> x0, matrix products: 10.9 us -> none  [the longest x1 5.52 us: body(): jnp.dot(low_gate, high_gate, preferred_element_type=jnp.float32)]
    ppermute x0 -> x4, waiting for transfers between devices: none -> 2.28 us  [the longest x2 2.27 us: body(): lax.ppermute(lows[which], 'fsdp', ring)]
    ppermute x0 -> x4, starting transfers between devices: none -> 1.15 us  [the longest x2 0.64 us: body(): lax.ppermute(trains[which], 'fsdp', ring)]
  transfers between devices with their start and end apart: 2 -> 4, of which waited for: 2 -> 1; matrix products, arithmetic and copies ran while one was open for 23% -> 0% of each run, Pallas kernels for 0% -> 65%
where the time goes in v2:
time: 36.8 us; the launch traced here: 36.5 us
  Pallas kernels  31.2 us (85%)
  waiting for transfers between devices  2.28 us (6%)
  local copies, waits for them, and re-layouts  1.21 us (3%)
  starting transfers between devices  1.15 us (3%)
  between operations  0.68 us (2%)
    pallas_call x3, Pallas kernels, place_pieces(): pl.pallas_call(functools.partial(piece_kernel, count, rows, columns, bloc...  23.5 us
    pallas_call x1, Pallas kernels, gather_gains(): pl.pallas_call(functools.partial(gain_kernel, sizes), out_shape=jax.Shape...  7.65 us
    ppermute x2, waiting for transfers between devices, body(): lax.ppermute(lows[which], 'fsdp', ring)  2.27 us
    unnamed x4, local copies, waits for them, and re-layouts  1.21 us
  transfers between devices with their start and end apart: 4, of which 1 were waited for; matrix products, arithmetic and copies ran while one was open for 0% of the time, Pallas kernels for 65%

profile of v2, /device:TPU:0, one launch (start us, length us, event | category | flops | bytes accessed | tf_op | source)
XLA Modules:
  0.0 36.5 jit_solution(7423218759176778133)
XLA Ops:
  0.6 0.6 %collective-permute-start = (bf16[1024,2048]{1,0:T(8,128)(2,1)}, bf16[1024,2048]{1,0:T(8,128)(2,1)}, u32[]{:S(2)}, u32[]{:S(2)}) collective-permute-start(bf16[1024,2048]{1,0:T(8,128)(2,1)} %refs_0_.1), channel_id=1, source_target_pairs={{0,16},{16,0},{1,17},{17,1},{2,18},{18,2},{3,19},{19,3},{4,20},{20... | collective-permute-start | bytes 12582920 | tf_op jit(solution)/shard_map/ppermute | solution.py:208
  1.2 0.1 collective-permute-start.2
  1.3 0.4 %collective-permute-start.1 = (bf16[32,1024]{1,0:T(8,128)(2,1)}, bf16[32,1024]{1,0:T(8,128)(2,1)S(1)}, u32[]{:S(2)}, u32[]{:S(2)}) collective-permute-start(bf16[32,1024]{1,0:T(8,128)(2,1)} %bitcast.7), channel_id=1, source_target_pairs={{0,16},{16,0},{1,17},{17,1},{2,18},{18,2},{3,19},{19,3},{4,20},{20... | collective-permute-start | bytes 196616 | tf_op jit(solution)/shard_map/ppermute | solution.py:207
  1.7 0.1 collective-permute-start.3
  1.8 10.3 %shard_map.103 = (bf16[2048,2048]{1,0:T(8,128)(2,1)}, bf16[2048,2048]{1,0:T(8,128)(2,1)}) custom-call(s32[1]{0:T(128)} %bitcast.2.at_ref, bf16[1024,2048]{1,0:T(8,128)(2,1)} %refs_0_.1, bf16[1024,2048]{1,0:T(8,128)(2,1)} %refs_1_.1, bf16[32,1024]{1,0:T(8,128)(2,1)} %bitcast.8, bf16[32,1024]{1,0:T(8,128)(2,1)} %bitcast.10, bf16[32,2048]{1,0:T(8,128)(2,1)} %refs_2_.2, ...), custom_call_target="tpu_custom_call" | custom-call | flops 268435456 | bytes 16777216 | tf_op jit(solution)/shard_map/pallas_call | solution.py:101
  12.0 2.3 %collective-permute-done.1.refs_1_ = bf16[32,1024]{1,0:T(8,128)(2,1)S(1)} collective-permute-done((bf16[32,1024]{1,0:T(8,128)(2,1)}, bf16[32,1024]{1,0:T(8,128)(2,1)S(1)}, u32[]{:S(2)}, u32[]{:S(2)}) %collective-permute-start.1) | collective-permute-done | bytes 65568 | tf_op jit(solution)/shard_map/ppermute | solution.py:207
  14.3 0.0 copy-start.1
  14.3 0.0 collective-permute-done.refs_0_
  14.3 0.6 %copy-done.1 = bf16[32,1024]{1,0:T(8,128)(2,1)} copy-done((bf16[32,1024]{1,0:T(8,128)(2,1)}, bf16[32,1024]{1,0:T(8,128)(2,1)S(1)}, u32[]{:S(2)}) %copy-start.1) | copy-done | bytes 65560
  14.9 6.0 %shard_map.104.after_ref = bf16[2048,2048]{1,0:T(8,128)(2,1)} custom-call(s32[1]{0:T(128)} %bitcast.at_ref, bf16[1024,2048]{1,0:T(8,128)(2,1)} %collective-permute-done.refs_0_, bf16[32,1024]{1,0:T(8,128)(2,1)} %copy-done.1, bf16[32,2048]{1,0:T(8,128)(2,1)} %refs_2_.2, bf16[2048,2048]{1,0:T(8,128)(2,1)} %get-tuple-element.7.refs_3_), custom_call_target="tpu_custom_call", output_to_operand_aliasing={{}: (4, {})} | custom-call | flops 134217728 | bytes 8388608 | tf_op jit(solution)/shard_map/pallas_call | solution.py:101
  20.9 7.7 %shard_map.105.refs_3_ = f32[8,2,2,128]{3,2,1,0:T(2,128)} custom-call(f32[2,128]{1,0:T(2,128)} %bitcast.11, f32[2,128]{1,0:T(2,128)} %bitcast.12, bf16[2048,2048]{1,0:T(8,128)(2,1)} %shard_map.104.after_ref), custom_call_target="tpu_custom_call" | custom-call | bytes 8000000 | tf_op jit(solution)/shard_map/pallas_call | solution.py:169
  28.6 0.0 collective-permute-done.3.refs_1_
  28.6 0.0 copy-start
  28.6 0.0 collective-permute-done.2.refs_0_
  28.6 0.6 %copy-done = bf16[32,1024]{1,0:T(8,128)(2,1)} copy-done((bf16[32,1024]{1,0:T(8,128)(2,1)}, bf16[32,1024]{1,0:T(8,128)(2,1)S(1)}, u32[]{:S(2)}) %copy-start) | copy-done | bytes 65560
  29.2 7.3 %shard_map.106 = (bf16[2048,2048]{1,0:T(8,128)(2,1)}, bf16[8,2,128]{2,1,0:T(2,128)(2,1)}) custom-call(s32[1]{0:T(128)} %bitcast.at_ref, bf16[1024,2048]{1,0:T(8,128)(2,1)} %collective-permute-done.2.refs_0_, bf16[32,1024]{1,0:T(8,128)(2,1)} %copy-done, bf16[32,2048]{1,0:T(8,128)(2,1)} %refs_2_.3, ...), custom_call_target="tpu_custom_call", output_to_operand_aliasing={{0}: (5, {})} | custom-call | flops 134217728 | bytes 8388608 | tf_op jit(solution)/shard_map/pallas_call | solution.py:101
Async XLA Ops:
  0.6 13.7 %collective-permute-start = (bf16[1024,2048]{1,0:T(8,128)(2,1)}, bf16[1024,2048]{1,0:T(8,128)(2,1)}, u32[]{:S(2)}, u32[]{:S(2)}) collective-permute-start(bf16[1024,2048]{1,0:T(8,128)(2,1)} %refs_0_.1), channel_id=1, source_target_pairs={{0,16},{16,0},{1,17},{17,1},{2,18},{18,2},{3,19},{19,3},{4,20},{20... | collective-permute-start | bytes 12582920 | tf_op jit(solution)/shard_map/ppermute | solution.py:208
  1.2 27.4 %collective-permute-start.2 = (bf16[1024,2048]{1,0:T(8,128)(2,1)}, bf16[1024,2048]{1,0:T(8,128)(2,1)}, u32[]{:S(2)}, u32[]{:S(2)}) collective-permute-start(bf16[1024,2048]{1,0:T(8,128)(2,1)} %refs_1_.1), channel_id=1, source_target_pairs={{0,16},{16,0},{1,17},{17,1},{2,18},{18,2},{3,19},{19,3},{4,20},{20... | collective-permute-start | bytes 12582920 | tf_op jit(solution)/shard_map/ppermute | solution.py:208
  1.3 13.0 %collective-permute-start.1 = (bf16[32,1024]{1,0:T(8,128)(2,1)}, bf16[32,1024]{1,0:T(8,128)(2,1)S(1)}, u32[]{:S(2)}, u32[]{:S(2)}) collective-permute-start(bf16[32,1024]{1,0:T(8,128)(2,1)} %bitcast.7), channel_id=1, source_target_pairs={{0,16},{16,0},{1,17},{17,1},{2,18},{18,2},{3,19},{19,3},{4,20},{20... | collective-permute-start | bytes 196616 | tf_op jit(solution)/shard_map/ppermute | solution.py:207
  1.7 26.9 %collective-permute-start.3 = (bf16[32,1024]{1,0:T(8,128)(2,1)}, bf16[32,1024]{1,0:T(8,128)(2,1)S(1)}, u32[]{:S(2)}, u32[]{:S(2)}) collective-permute-start(bf16[32,1024]{1,0:T(8,128)(2,1)} %bitcast.9), channel_id=1, source_target_pairs={{0,16},{16,0},{1,17},{17,1},{2,18},{18,2},{3,19},{19,3},{4,20},{20... | collective-permute-start | bytes 196616 | tf_op jit(solution)/shard_map/ppermute | solution.py:207
  14.3 0.6 %copy-start.1 = (bf16[32,1024]{1,0:T(8,128)(2,1)}, bf16[32,1024]{1,0:T(8,128)(2,1)S(1)}, u32[]{:S(2)}) copy-start(bf16[32,1024]{1,0:T(8,128)(2,1)S(1)} %collective-permute-done.1.refs_1_) | copy-start | bytes 196612
  28.6 0.6 %copy-start = (bf16[32,1024]{1,0:T(8,128)(2,1)}, bf16[32,1024]{1,0:T(8,128)(2,1)S(1)}, u32[]{:S(2)}) copy-start(bf16[32,1024]{1,0:T(8,128)(2,1)S(1)} %collective-permute-done.3.refs_1_) | copy-start | bytes 196612
